TPU v7x, 128 devices: a whole 4x4x4 slice. The times are simulated.
128 devices in a mesh: ep: 8 (over z_lo, x), fsdp: 16 (over z_hi, y, core).
Axes of the slice: x: 4, y: 4, z: 4 (z_hi: 2, z_lo: 2; z = z_hi * 2 + z_lo), core: 2. Of those that a mesh axis runs over, the one named last changes fastest.
Arguments:
- train_gate: float32 [64, 2048, 1408], P('ep', 'fsdp'), may hold values from -0.1875 to 0.1875
- other_gate: bfloat16 [64, 2048, 1408], P('ep', 'fsdp'), may hold values from -0.0625 to 0.0625
- train_up: float32 [64, 2048, 1408], P('ep', 'fsdp'), may hold values from -0.1875 to 0.1875
- other_up: bfloat16 [64, 2048, 1408], P('ep', 'fsdp'), may hold values from -0.0625 to 0.0625
- router_weight: float32 [2048, 64], P('fsdp', 'ep'), may hold values from -0.125 to 0.125
- router_gain: float32 [2048], P('fsdp'), may hold values from 0.25 to 1.75
Outputs:
- ready_gate: bfloat16 [64, 2048, 1408], P('ep', None, 'fsdp')
- ready_up: bfloat16 [64, 2048, 1408], P('ep', None, 'fsdp')
- scale_gate: float32 [64, 1408], P('ep', 'fsdp')
- scale_up: float32 [64, 1408], P('ep', 'fsdp')
- serve_router: bfloat16 [2048, 64], replicated
All inputs are finite; a program needn't handle non-finite values. Where the computation divides by a largest or mean magnitude, that divisor is 1e-20 or more.
Results may differ from a plain program's by a relative error of at most 0.001.
Values may be sent and summed in bfloat16 or wider, within the bound.
A program may use at most 128 MiB of HBM per device.

v0:
```python
import jax
import jax.numpy as jnp
from jax import lax
from jax.sharding import Mesh
from jax.sharding import PartitionSpec as P

EP = ("ep_0", "ep_1")


def sent_to_all(array, axis):
    peers = lax.axis_size(axis)
    return lax.all_to_all(
        jnp.broadcast_to(array[None], (peers, *array.shape)), axis, 0, 0, tiled=True
    )


def taken_together(array, axis):
    everything = sent_to_all(array, axis)
    return jnp.max(everything, axis=0)


def in_one(arrays, axis):
    flat, at, finished = (jnp.concatenate([a.reshape(-1) for a in arrays]), 0, [])
    total = taken_together(flat, axis)
    for a in arrays:
        finished.append(total[at : at + a.size].reshape(a.shape))
        at += a.size
    return tuple(finished)


def side_by_side(arrays, axis, split_dim, concat_dim, along):
    widths = [a.shape[along] for a in arrays]
    both = jnp.concatenate(arrays, axis=along)
    filled = lax.all_to_all(both, axis, split_axis=split_dim, concat_axis=concat_dim, tiled=True)
    return tuple(jnp.split(filled, [sum(widths[:k]) for k in range(1, len(widths))], axis=along))


def joined_along(parts, dim):
    lengths = list(parts.shape[1:])
    lengths[dim] *= parts.shape[0]
    return jnp.moveaxis(parts, 0, dim).reshape(lengths)


def gathered_copies(array, axis, dim):
    parts = sent_to_all(array, axis)
    return joined_along(parts, dim)


def stacked_from(array, axes, order):
    parts = array[None]
    for k in order:
        parts = lax.all_gather(parts, axes[k], axis=0, tiled=True)
    carried = [lax.axis_size(axes[k]) for k in reversed(order)]
    parts = parts.reshape(*carried, *array.shape)
    turned = sorted(range(len(order)), key=lambda place: order[len(order) - 1 - place])
    return parts.transpose(*turned, *range(len(order), parts.ndim)).reshape(-1, *array.shape)


def gather_axes(array, axes, order, dim):
    return joined_along(stacked_from(array, axes, order), dim)


def per_device(train_gate, other_gate, train_up, other_up, router_weight, router_gain):
    latest_gate = train_gate + other_gate.astype(jnp.float32)
    latest_up = train_up + other_up.astype(jnp.float32)
    scale_gate, scale_up = in_one(
        (jnp.max(jnp.abs(latest_gate), axis=1), jnp.max(jnp.abs(latest_up), axis=1)), "fsdp"
    )
    narrow_gate, narrow_up = (
        (latest_gate / jnp.expand_dims(scale_gate, 1)).astype(jnp.bfloat16),
        (latest_up / jnp.expand_dims(scale_up, 1)).astype(jnp.bfloat16),
    )
    ready_gate, ready_up = side_by_side((narrow_gate, narrow_up), "fsdp", 2, 1, 0)
    scale_gate = lax.dynamic_slice_in_dim(
        scale_gate, lax.axis_index("fsdp") * ready_gate.shape[2], ready_gate.shape[2], axis=1
    )
    scale_up = lax.dynamic_slice_in_dim(
        scale_up, lax.axis_index("fsdp") * ready_up.shape[2], ready_up.shape[2], axis=1
    )
    part_router = (router_weight * router_gain[:, None]).astype(jnp.bfloat16)
    row_router = gathered_copies(part_router, "fsdp", 0)
    serve_router = gather_axes(row_router, EP, (0, 1), 1)
    return (ready_gate, ready_up, scale_gate, scale_up, serve_router)


def solution(mesh):
    split = Mesh(mesh.devices.reshape(2, 4, mesh.shape["fsdp"]), ("ep_0", "ep_1", "fsdp"))
    return jax.shard_map(
        per_device,
        mesh=split,
        in_specs=(
            P(EP, "fsdp", None),
            P(EP, "fsdp", None),
            P(EP, "fsdp", None),
            P(EP, "fsdp", None),
            P("fsdp", EP),
            P("fsdp"),
        ),
        out_specs=(P(EP, None, "fsdp"), P(EP, None, "fsdp"), P(EP, "fsdp"), P(EP, "fsdp"), P()),
        check_vma=False,
    )
```

profile of v0, /device:TPU:1, one launch (start us, length us, event | category | flops | bytes accessed | tf_op | source)
XLA Modules:
  0.0 182.0 jit_solution(4989648456742953288)
XLA Ops:
  0.6 6.5 %copy.69 = f32[8,128,1408]{1,0,2:T(8,128)} copy(f32[8,128,1408]{2,1,0:T(8,128)} %param.6) | data formatting | bytes 11534336 | tf_op args[0]
  7.1 4.1 %copy.68 = bf16[8,128,1408]{1,0,2:T(8,128)(2,1)S(1)} copy(bf16[8,128,1408]{2,1,0:T(8,128)(2,1)} %param.7) | data formatting | bytes 5767168 | tf_op args[1]
  11.2 5.1 %abs_reduce_fusion.1 = f32[8,1408]{0,1:T(8,128)} fusion(f32[8,128,1408]{1,0,2:T(8,128)} %copy.69, bf16[8,128,1408]{1,0,2:T(8,128)(2,1)S(1)} %copy.68), kind=kLoop, calls=%fused_computation.5 | loop fusion | flops 5755904 | bytes 8695808 | tf_op jit(solution)/shard_map/reduce_max | solution.py:67
  16.3 1.3 copy.70
  17.6 6.5 %copy.72 = f32[8,128,1408]{1,0,2:T(8,128)} copy(f32[8,128,1408]{2,1,0:T(8,128)} %param.8) | data formatting | bytes 11534336 | tf_op args[2]
  24.1 4.9 %copy.71 = bf16[8,128,1408]{1,0,2:T(8,128)(2,1)} copy(bf16[8,128,1408]{2,1,0:T(8,128)(2,1)} %param.9) | data formatting | bytes 5767168 | tf_op args[3]
  29.0 5.6 %abs_reduce_fusion = f32[8,1408]{0,1:T(8,128)} fusion(f32[8,128,1408]{1,0,2:T(8,128)} %copy.72, bf16[8,128,1408]{1,0,2:T(8,128)(2,1)} %copy.71), kind=kLoop, calls=%fused_computation.3 | loop fusion | flops 5755904 | bytes 8695808 | tf_op jit(solution)/shard_map/reduce_max | solution.py:67
  34.6 1.3 copy.73
  35.9 1.8 %broadcast_in_dim.4 = f32[16,1,22528]{2,1,0:T(1,128)} broadcast(f32[22528]{0:T(1024)S(1)} %pad_maximum_fusion.1), dimensions={2} | broadcast | bytes 1531904 | tf_op jit(solution)/shard_map/broadcast_in_dim | solution.py:13
  37.8 9.3 %all-to-all-start = ((f32[16,1,22528]{2,1,0:T(1,128)}), f32[16,1,22528]{2,1,0:T(1,128)}, u32[]{:S(2)}, u32[]{:S(2)}) async-start(f32[16,1,22528]{2,1,0:T(1,128)} %broadcast_in_dim.4), calls=%async_computation | async-start | bytes 2883584 | tf_op jit(solution)/shard_map/all_to_all | solution.py:12
  47.1 21.6 %all-to-all-done = f32[16,1,22528]{2,1,0:T(1,128)} async-done(((f32[16,1,22528]{2,1,0:T(1,128)}), f32[16,1,22528]{2,1,0:T(1,128)}, u32[]{:S(2)}, u32[]{:S(2)}) %all-to-all-start) | async-done | bytes 1441824 | tf_op jit(solution)/shard_map/all_to_all | solution.py:12
  69.3 4.1 %all-to-all-start.2 = ((bf16[16,128,8]{1,2,0:T(8,128)(2,1)}), bf16[16,128,8]{1,2,0:T(8,128)(2,1)S(1)}, u32[]{:S(2)}, u32[]{:S(2)}) async-start(bf16[16,128,8]{1,2,0:T(8,128)(2,1)} %broadcast_in_dim.5), calls=%async_computation.2 | async-start | bytes 65536 | tf_op jit(solution)/shard_map/all_to_all | solution.py:12
  73.3 2.3 %reduce_max.29 = f32[22528]{0:T(1024)S(1)} reduce(f32[16,1,22528]{2,1,0:T(1,128)} %all-to-all-done, f32[]{:T(128)} %constant.5.clone.1), dimensions={0,1}, to_apply=%region_2.0 | reduce | flops 337920 | bytes 1531908 | tf_op jit(solution)/shard_map/reduce_max | solution.py:19
  75.6 1.1 copy.75
  76.8 1.1 copy.76
  77.9 6.8 %divide_convert_fusion = (bf16[8,128,1408]{1,0,2:T(8,128)(2,1)S(1)}, bf16[8,128,1408]{1,0,2:T(8,128)(2,1)S(1)}) fusion(f32[8,128,1408]{1,0,2:T(8,128)} %copy.72, bf16[8,128,1408]{1,0,2:T(8,128)(2,1)} %copy.71, f32[8,1408]{0,1:T(8,128)} %copy.76, f32[8,1408]{0,1:T(8,128)} %copy.75, f32[8,128,1408]{1,0,2:T(8,128)} %copy.69, bf16[8,128,1408]{1,0,2:T(8,128)(2,1)S(1)} %copy.68), kind=kLoop, calls=%fused_computation.1 | loop fusion | flops 11534336 | bytes 23158784 | tf_op jit(solution)/shard_map/convert_element_type | solution.py:71
  84.7 3.2 %pad_maximum_fusion = bf16[16,128,1408]{1,0,2:T(8,128)(2,1)} fusion(bf16[8,128,1408]{1,0,2:T(8,128)(2,1)S(1)} %get-tuple-element.9, bf16[8,128,1408]{1,0,2:T(8,128)(2,1)S(1)} %get-tuple-element.10), kind=kLoop, calls=%fused_computation | loop fusion | flops 11534336 | bytes 11534336 | tf_op jit(solution)/shard_map/concatenate | solution.py:33
  88.0 7.3 %all-to-all-start.1 = ((bf16[16,128,1408]{1,0,2:T(8,128)(2,1)}), bf16[16,128,1408]{1,0,2:T(8,128)(2,1)}, u32[]{:S(2)}, u32[]{:S(2)}) async-start(bf16[16,128,1408]{1,0,2:T(8,128)(2,1)} %pad_maximum_fusion), calls=%async_computation.1 | async-start | bytes 11534336 | tf_op jit(solution)/shard_map/all_to_all | solution.py:34
  95.3 57.5 %all_gather.6 = bf16[2,2048,8]{1,2,0:T(8,128)(2,1)S(1)} all-gather(bf16[1,2048,8]{1,2,0:T(8,128)(2,1)S(1)} %bitcast.27), channel_id=1, replica_groups=mesh['ep_0'=2,'ep_1'=4,'fsdp'=16] {'ep_0'}, dimensions={0}, use_global_device_ids=true | all-gather | bytes 98304 | tf_op jit(solution)/shard_map/all_gather | solution.py:52
  152.7 10.9 %all_gather.7 = bf16[8,2048,8]{1,2,0:T(8,128)(2,1)S(1)} all-gather(bf16[2,2048,8]{1,2,0:T(8,128)(2,1)S(1)} %all_gather.6), channel_id=1, replica_groups=mesh['ep_0'=2,'ep_1'=4,'fsdp'=16] {'ep_1'}, dimensions={0}, use_global_device_ids=true | all-gather | bytes 327680 | tf_op jit(solution)/shard_map/all_gather | solution.py:52
  165.0 7.1 %all-to-all-done.1 = bf16[16,128,1408]{1,0,2:T(8,128)(2,1)} async-done(((bf16[16,128,1408]{1,0,2:T(8,128)(2,1)}), bf16[16,128,1408]{1,0,2:T(8,128)(2,1)}, u32[]{:S(2)}, u32[]{:S(2)}) %all-to-all-start.1) | async-done | bytes 5767200 | tf_op jit(solution)/shard_map/all_to_all | solution.py:34
  172.1 4.1 %copy.77 = bf16[16,128,1408]{1,2,0:T(8,128)(2,1)S(1)} copy(bf16[16,128,1408]{1,0,2:T(8,128)(2,1)} %all-to-all-done.1) | data formatting | bytes 11534336 | tf_op jit(solution)/shard_map/all_to_all | solution.py:34
  177.3 2.4 %copy.88 = bf16[8,16,11,8,128]{4,3,1,2,0:T(8,128)(2,1)} copy(bf16[8,16,11,8,128]{4,3,2,1,0:T(8,128)(2,1)S(1)} %get-tuple-element.5) | data formatting | bytes 5767168 | tf_op jit(solution)/shard_map/split | solution.py:35
  179.6 2.4 %copy.89 = bf16[8,16,11,8,128]{4,3,1,2,0:T(8,128)(2,1)} copy(bf16[8,16,11,8,128]{4,3,2,1,0:T(8,128)(2,1)S(1)} %get-tuple-element.6) | data formatting | bytes 5767168 | tf_op jit(solution)/shard_map/split | solution.py:35
  (16 shorter events, 3.1 us)
Async XLA Ops:
  29.0 18.1 %copy-start = (f32[128,8]{0,1:T(8,128)S(1)}, f32[128,8]{0,1:T(8,128)}, u32[]{:S(2)}) copy-start(f32[128,8]{0,1:T(8,128)} %param.10) | copy-start | bytes 12292
  29.0 18.1 %copy-start.1 = (f32[128]{0:T(128)S(1)}, f32[128]{0:T(128)}, u32[]{:S(2)}) copy-start(f32[128]{0:T(128)} %param.11) | copy-start | bytes 1540
  37.8 30.9 %all-to-all-start = ((f32[16,1,22528]{2,1,0:T(1,128)}), f32[16,1,22528]{2,1,0:T(1,128)}, u32[]{:S(2)}, u32[]{:S(2)}) async-start(f32[16,1,22528]{2,1,0:T(1,128)} %broadcast_in_dim.4), calls=%async_computation | async-start | bytes 2883584 | tf_op jit(solution)/shard_map/all_to_all | solution.py:12
  69.3 18.7 %all-to-all-start.2 = ((bf16[16,128,8]{1,2,0:T(8,128)(2,1)}), bf16[16,128,8]{1,2,0:T(8,128)(2,1)S(1)}, u32[]{:S(2)}, u32[]{:S(2)}) async-start(bf16[16,128,8]{1,2,0:T(8,128)(2,1)} %broadcast_in_dim.5), calls=%async_computation.2 | async-start | bytes 65536 | tf_op jit(solution)/shard_map/all_to_all | solution.py:12
  88.0 84.2 %all-to-all-start.1 = ((bf16[16,128,1408]{1,0,2:T(8,128)(2,1)}), bf16[16,128,1408]{1,0,2:T(8,128)(2,1)}, u32[]{:S(2)}, u32[]{:S(2)}) async-start(bf16[16,128,1408]{1,0,2:T(8,128)(2,1)} %pad_maximum_fusion), calls=%async_computation.1 | async-start | bytes 11534336 | tf_op jit(solution)/shard_map/all_to_all | solution.py:34
where the time goes:
time: 184 us; the launch traced here: 182 us
  blocking collectives  68.4 us (37%)
  local copies, waits for them, and re-layouts  40.6 us (22%)
  waiting for transfers between devices  28.7 us (16%)
  other arithmetic  23 us (12%)
  starting transfers between devices  20.7 us (11%)
    all_gather x2, blocking collectives, stacked_from(): parts = lax.all_gather(parts, axes[k], axis=0, tiled=True)  68.4 us
    unnamed x9, local copies, waits for them, and re-layouts  22.9 us
    all_to_all x2, waiting for transfers between devices, sent_to_all(): lax.all_to_all(jnp.broadcast_to(array[None], (peers, *array.shape)), axis...  21.6 us
    all_to_all x2, starting transfers between devices, sent_to_all(): lax.all_to_all(jnp.broadcast_to(array[None], (peers, *array.shape)), axis...  13.4 us
    all_to_all x1, starting transfers between devices, side_by_side(): lax.all_to_all(both, axis, split_axis=split_dim, concat_axis=concat_dim,...  7.3 us
    all_to_all x1, waiting for transfers between devices, side_by_side(): lax.all_to_all(both, axis, split_axis=split_dim, concat_axis=concat_dim,...  7.13 us
    convert_element_type x1, other arithmetic, per_device(): (latest_up / jnp.expand_dims(scale_up, 1)).astype(jnp.bfloat16)  6.79 us
    reduce_max x1, other arithmetic, per_device(): jnp.max(jnp.abs(latest_up), axis=1)  5.58 us
  transfers between devices with their start and end apart: 3, of which 2 were waited for; matrix products, arithmetic and copies ran while one was open for 9% of the time, Pallas kernels for 0%

commit v1 on v0

v1 whole, which is shorter than its diff:
```python
import functools

import jax
import jax.numpy as jnp
from jax import lax
from jax.experimental import pallas as pl
from jax.experimental.pallas import tpu as pltpu
from jax.sharding import Mesh
from jax.sharding import PartitionSpec as P

MESH = pl.DeviceIdType.MESH
AXES = ("zl", "x", "zh", "y", "c")
EP = ("zl", "x")
FSDP = ("zh", "y", "c")
LANES = 128
PEERS = (
    (1, 1, 0), (3, 1, 0), (0, 1, 0), (2, 1, 0), (1, 0, 0), (3, 0, 0), (2, 0, 0),
    (1, 1, 1), (3, 1, 1), (0, 1, 1), (2, 1, 1), (1, 0, 1), (3, 0, 1), (2, 0, 1), (0, 0, 1),
)


def kernel(
    sizes,
    tg, og, tu, ou, rw, rg,
    gate, up, sg, su, router,
    train, other, turned, blocks, first, firsts, local, parts, scales, tile,
    load_sem, send_sem, recv_sem, own_sem,
    first_send, first_recv, part_send, part_recv, scale_send, scale_recv,
    tile_send, tile_recv, pair_send, pair_recv, row_send, row_recv,
):
    nzl, nx, nzh, ny, nc = sizes
    experts, depth, width = tg.shape
    members = nzh * ny * nc
    cut = width // members
    strips = width // LANES
    zl, x, zh, y, c = (lax.axis_index(a) for a in AXES)
    me = (zh * ny + y) * nc + c
    part = zl * nx + x
    arrays = ((tg, og, gate), (tu, ou, up))

    def load(t, e):
        return (
            pltpu.make_async_copy(arrays[t][0].at[e], train.at[t, e], load_sem.at[0, t, e]),
            pltpu.make_async_copy(arrays[t][1].at[e], other.at[t, e], load_sem.at[1, t, e]),
        )

    def peer(step):
        dy, dz, dc = step
        ty, tz, tc = lax.rem(y + dy, ny), lax.rem(zh + dz, nzh), lax.rem(c + dc, nc)
        return (tz * ny + ty) * nc + tc, (zl, x, tz, ty, tc)

    others = [peer(step) for step in PEERS]
    across = (lax.rem(zl + 1, nzl), x, zh, y, c)
    along = [(zl, lax.rem(x + k, nx), zh, y, c) for k in range(1, nx)]
    mine = pl.ds(pl.multiple_of(me * LANES, LANES), LANES)

    barrier = pltpu.get_barrier_semaphore()
    everyone = [d for _, d in others] + [across] + along
    for d in everyone:
        pl.semaphore_signal(barrier, inc=1, device_id=d, device_id_type=MESH)

    for t in range(2):
        for copy in load(t, 0):
            copy.start()

    @pl.loop(1, experts)
    def _(e):
        for t in range(2):
            for copy in load(t, e):
                copy.start()

    def largest(t, e):
        for copy in load(t, e):
            copy.wait()
        latest = train[t, e] + other[t, e].astype(jnp.float32)
        return jnp.max(jnp.abs(latest), axis=0, keepdims=True)

    for t in range(2):
        top = largest(t, 0)
        for k in range(strips):
            first[t, k : k + 1, :] = top[:, k * LANES : (k + 1) * LANES]
    tile[...] = (rw[...] * rg[...]).astype(tile.dtype)
    firsts[me] = first[...]

    pl.semaphore_wait(barrier, len(everyone))
    for _, d in others:
        pltpu.make_async_remote_copy(
            first, firsts.at[me], first_send, first_recv, device_id=d, device_id_type=MESH
        ).start()
    rows = pl.ds(pl.multiple_of(part * 8, 8), 8)
    for _, d in others:
        pltpu.make_async_remote_copy(
            tile, router.at[rows, mine], tile_send, tile_recv, device_id=d, device_id_type=MESH
        ).start()
    pltpu.make_async_copy(tile, router.at[rows, mine], own_sem.at[1]).start()

    @pl.loop(1, experts)
    def _(e):
        for t in range(2):
            chunk = t * experts + e
            top = largest(t, e)
            for k in range(strips):
                local[chunk, k : k + 1, :] = top[:, k * LANES : (k + 1) * LANES]
            owner = chunk
            home = (zl, x, owner // (ny * nc), lax.rem(owner // nc, ny), lax.rem(owner, nc))

            @pl.when(owner != me)
            def _():
                pltpu.make_async_remote_copy(
                    local.at[chunk], parts.at[me], part_send, part_recv,
                    device_id=home, device_id_type=MESH,
                ).start()

            @pl.when(owner == me)
            def _():
                parts[me] = local[chunk]

    def send(t, e):
        chunk = t * experts + e
        scale = scales[chunk]
        inverse = 1.0 / scale
        for k in range(strips):
            lanes = slice(k * LANES, (k + 1) * LANES)
            latest = train[t, e, :, lanes] + other[t, e, :, lanes].astype(jnp.float32)
            turned[t, lanes, :] = (latest * inverse[k : k + 1, :]).T
        for p in range(members):
            blocks[p, chunk] = turned[t, p * cut : (p + 1) * cut, :].astype(blocks.dtype)
        for p, d in others:
            pltpu.make_async_remote_copy(
                blocks.at[p, chunk], arrays[t][2].at[e, :, mine], send_sem, recv_sem,
                device_id=d, device_id_type=MESH,
            ).start()
        pltpu.make_async_copy(
            blocks.at[me, chunk], arrays[t][2].at[e, :, mine], own_sem.at[0]
        ).start()

    got = firsts.at[pl.ds(0, members - 1)]
    pltpu.make_async_copy(got, got, first_recv).wait()
    for t in range(2):
        scales[t * experts] = jnp.max(firsts[:, t], axis=0)
    send(0, 0)

    row = router.at[rows, pl.ds(0, (members - 1) * LANES)]
    pltpu.make_async_copy(row, row, tile_recv).wait()
    pltpu.make_async_copy(tile, router.at[rows, mine], own_sem.at[1]).wait()
    pltpu.make_async_remote_copy(
        router.at[rows], router.at[rows], pair_send, pair_recv, device_id=across, device_id_type=MESH
    ).start()

    owns = lax.rem(me, experts) != 0

    @pl.when(owns)
    def _():
        got = parts.at[pl.ds(0, members - 1)]
        pltpu.make_async_copy(got, got, part_recv).wait()
        scales[me] = jnp.max(parts[...], axis=0)
        for _, d in others:
            pltpu.make_async_remote_copy(
                scales.at[me], scales.at[me], scale_send, scale_recv.at[me],
                device_id=d, device_id_type=MESH,
            ).start()

    send(1, 0)

    pltpu.make_async_remote_copy(
        router.at[rows], router.at[rows], pair_send, pair_recv, device_id=across, device_id_type=MESH
    ).wait()
    for d in along:
        for h in range(nzl):
            block = pl.ds(pl.multiple_of((h * nx + x) * 8, 8), 8)
            pltpu.make_async_remote_copy(
                router.at[block], router.at[block], row_send, row_recv, device_id=d, device_id_type=MESH
            ).start()

    @pl.loop(1, experts)
    def _(e):
        for t in range(2):
            chunk = t * experts + e

            @pl.when(chunk != me)
            def _():
                pltpu.make_async_copy(
                    scales.at[chunk], scales.at[chunk], scale_recv.at[chunk]
                ).wait()

            send(t, e)

    for t, out in enumerate((sg, su)):
        whole = jnp.concatenate(
            [scales[t * experts : (t + 1) * experts, k, :] for k in range(strips)], axis=1
        )
        for p in range(members):

            @pl.when(me == p)
            def _(out=out, whole=whole, p=p):
                out[...] = whole[:, p * cut : (p + 1) * cut]

    def drain(ref, sem):
        pltpu.make_async_copy(ref, ref, sem).wait()

    drain(firsts.at[pl.ds(0, members - 1)], first_send)
    row = router.at[pl.ds(0, 8), pl.ds(0, (members - 1) * LANES)]
    drain(row, tile_send)

    @pl.when(owns)
    def _():
        drain(local.at[pl.ds(0, members - 3)], part_send)
        drain(firsts.at[pl.ds(0, members - 1), 0], scale_send)

    @pl.when(jnp.logical_not(owns))
    def _():
        drain(local.at[pl.ds(0, members - 2)], part_send)

    count = nzl * (nx - 1) * 8
    drain(router.at[pl.ds(0, count)], row_send)
    drain(router.at[pl.ds(0, count)], row_recv)
    drain(blocks.at[0], own_sem.at[0])
    drain(blocks.at[pl.ds(0, members - 1)], send_sem)
    drain(blocks.at[pl.ds(0, members - 1)], recv_sem)


def per_device(sizes, train_gate, other_gate, train_up, other_up, router_weight, router_gain):
    experts, depth, width = train_gate.shape
    members = sizes[2] * sizes[3] * sizes[4]
    parts = sizes[0] * sizes[1]
    cut = width // members
    strips = width // LANES
    chunks = 2 * experts
    dma, bf16, f32 = pltpu.SemaphoreType.DMA, jnp.bfloat16, jnp.float32
    hbm = pl.BlockSpec(memory_space=pl.ANY)
    vmem = pl.BlockSpec(memory_space=pltpu.VMEM)
    gate, up, sg, su, router = pl.pallas_call(
        functools.partial(kernel, sizes),
        out_shape=(
            jax.ShapeDtypeStruct((experts, cut, depth * members), bf16),
            jax.ShapeDtypeStruct((experts, cut, depth * members), bf16),
            jax.ShapeDtypeStruct((experts, cut), f32),
            jax.ShapeDtypeStruct((experts, cut), f32),
            jax.ShapeDtypeStruct((8 * parts, depth * members), bf16),
        ),
        in_specs=[hbm] * 4 + [vmem] * 2,
        out_specs=(hbm, hbm, vmem, vmem, hbm),
        scratch_shapes=[
            pltpu.VMEM((2, experts, depth, width), f32),
            pltpu.VMEM((2, experts, depth, width), bf16),
            pltpu.VMEM((2, width, depth), f32),
            pltpu.VMEM((members, chunks, cut, depth), bf16),
            pltpu.VMEM((2, strips, LANES), f32),
            pltpu.VMEM((members, 2, strips, LANES), f32),
            pltpu.VMEM((chunks, strips, LANES), f32),
            pltpu.VMEM((members, strips, LANES), f32),
            pltpu.VMEM((chunks, strips, LANES), f32),
            pltpu.VMEM((8, depth), bf16),
            dma((2, 2, experts)),
            dma, dma, dma((2,)),
            dma, dma, dma, dma, dma, dma((chunks,)),
            dma, dma, dma, dma, dma, dma,
        ],
        compiler_params=pltpu.CompilerParams(
            collective_id=0, has_side_effects=True, vmem_limit_bytes=40 * 2**20
        ),
        name="regroup",
    )(train_gate, other_gate, train_up, other_up, router_weight.T, router_gain[None])
    return gate.transpose(0, 2, 1), up.transpose(0, 2, 1), sg, su, router.T


def solution(mesh):
    sizes = (2, mesh.shape["ep"] // 2, 2, mesh.shape["fsdp"] // 4, 2)
    split = Mesh(mesh.devices.reshape(sizes), AXES)
    return jax.shard_map(
        functools.partial(per_device, sizes),
        mesh=split,
        in_specs=(
            P(EP, FSDP, None),
            P(EP, FSDP, None),
            P(EP, FSDP, None),
            P(EP, FSDP, None),
            P(FSDP, EP),
            P(FSDP),
        ),
        out_specs=(P(EP, None, FSDP), P(EP, None, FSDP), P(EP, FSDP), P(EP, FSDP), P()),
        check_vma=False,
    )
```

time: 184 us -> 92.2 us (0.50)
  Pallas kernels: 0 us -> 81.3 us
  blocking collectives: 68.4 us -> 0 us
  local copies, waits for them, and re-layouts: 40.6 us -> 10 us
  waiting for transfers between devices: 28.7 us -> 0 us
  other arithmetic: 23 us -> 0 us
  starting transfers between devices: 20.7 us -> 0 us
    pallas_call x0 -> x1, Pallas kernels: none -> 81.3 us  [per_device(): pl.pallas_call(functools.partial(kernel, sizes), out_shape=(jax.ShapeDtyp...]
    all_gather x2 -> x0, blocking collectives: 68.4 us -> none  [stacked_from(): parts = lax.all_gather(parts, axes[k], axis=0, tiled=True)]
    all_to_all x3 -> x0, waiting for transfers between devices: 28.7 us -> none  [the longest x2 21.6 us: sent_to_all(): lax.all_to_all(jnp.broadcast_to(array[None], (peers, *array.shape)), axis...]
    all_to_all x3 -> x0, starting transfers between devices: 20.7 us -> none  [the longest x2 13.4 us: sent_to_all(): lax.all_to_all(jnp.broadcast_to(array[None], (peers, *array.shape)), axis...]
    reduce_max x3 -> x0, other arithmetic: 12.9 us -> none  [the longest x1 5.58 us: per_device(): jnp.max(jnp.abs(latest_up), axis=1)]
    unnamed x9 -> x13, local copies, waits for them, and re-layouts: 22.9 us -> 10 us
    convert_element_type x2 -> x0, other arithmetic: 6.8 us -> none  [the longest x1 6.79 us: per_device(): (latest_up / jnp.expand_dims(scale_up, 1)).astype(jnp.bfloat16)]
    split x2 -> x0, local copies, waits for them, and re-layouts: 4.76 us -> none  [side_by_side(): jnp.split(filled, [sum(widths[:k]) for k in range(1, len(widths))], axis=...]
  transfers between devices with their start and end apart: 3 -> 0, of which waited for: 2 -> 0; matrix products, arithmetic and copies ran while one was open for 9% -> 0% of each run, Pallas kernels for 0% -> 0%
where the time goes in v1:
time: 92.2 us; the launch traced here: 92 us
  Pallas kernels  81.3 us (88%)
  local copies, waits for them, and re-layouts  10 us (11%)
    pallas_call x1, Pallas kernels, per_device(): pl.pallas_call(functools.partial(kernel, sizes), out_shape=(jax.ShapeDtyp...  81.3 us
    unnamed x13, local copies, waits for them, and re-layouts  10 us

profile of v1, /device:TPU:1, one launch (start us, length us, event | category | flops | bytes accessed | tf_op | source)
XLA Modules:
  0.0 92.0 jit_solution(12247056753221839899)
XLA Ops:
  0.6 0.0 copy-start
  0.6 1.8 %copy-done = bf16[8,128,1408]{2,1,0:T(8,128)(2,1)S(1)} copy-done((bf16[8,128,1408]{2,1,0:T(8,128)(2,1)S(1)}, bf16[8,128,1408]{2,1,0:T(8,128)(2,1)}, u32[]{:S(2)}) %copy-start) | copy-done | bytes 2883608
  2.4 0.0 copy-start.1
  2.5 1.8 %copy-done.1 = bf16[8,128,1408]{2,1,0:T(8,128)(2,1)S(1)} copy-done((bf16[8,128,1408]{2,1,0:T(8,128)(2,1)S(1)}, bf16[8,128,1408]{2,1,0:T(8,128)(2,1)}, u32[]{:S(2)}) %copy-start.1) | copy-done | bytes 2883608
  4.3 0.0 copy-start.2
  4.3 0.7 copy-done.2
  5.0 0.0 copy-start.3
  5.0 0.7 copy-done.3
  5.6 81.3 %regroup.1 = (bf16[8,88,2048]{2,1,0:T(8,128)(2,1)S(1)}, bf16[8,88,2048]{2,1,0:T(8,128)(2,1)S(1)}, f32[8,88]{1,0:T(8,128)S(1)}, f32[8,88]{1,0:T(8,128)S(1)}, bf16[64,2048]{1,0:T(8,128)(2,1)S(1)}) custom-call(f32[8,128,1408]{2,1,0:T(8,128)} %tg.1, bf16[8,128,1408]{2,1,0:T(8,128)(2,1)S(1)} %copy-done, f32[8,128,1408]{2,1,0:T(8,128)} %tu.1, ...), custom_call_target="tpu_custom_call" | custom-call | tf_op jit(solution)/shard_map/regroup/pallas_call | solution.py:232
  86.9 1.6 %copy.16 = bf16[8,2048,88]{1,2,0:T(8,128)(2,1)} copy(bf16[8,2048,88]{1,2,0:T(8,128)(2,1)S(1)} %bitcast.6) | data formatting | bytes 5767168
  88.5 1.6 %copy.17 = bf16[8,2048,88]{1,2,0:T(8,128)(2,1)} copy(bf16[8,2048,88]{1,2,0:T(8,128)(2,1)S(1)} %bitcast.5) | data formatting | bytes 5767168
  90.1 0.6 copy.18
  90.7 0.6 copy.19
  91.3 0.7 copy.20
Async XLA Ops:
  0.6 1.8 %copy-start = (bf16[8,128,1408]{2,1,0:T(8,128)(2,1)S(1)}, bf16[8,128,1408]{2,1,0:T(8,128)(2,1)}, u32[]{:S(2)}) copy-start(bf16[8,128,1408]{2,1,0:T(8,128)(2,1)} %og.1) | copy-start | bytes 8650756
  2.4 1.8 %copy-start.1 = (bf16[8,128,1408]{2,1,0:T(8,128)(2,1)S(1)}, bf16[8,128,1408]{2,1,0:T(8,128)(2,1)}, u32[]{:S(2)}) copy-start(bf16[8,128,1408]{2,1,0:T(8,128)(2,1)} %ou.1) | copy-start | bytes 8650756
  4.3 0.7 copy-start.2
  5.0 0.7 copy-start.3

commit v2 on v1

--- a/solution.py
+++ b/solution.py
@@ -23,8 +23,8 @@
     sizes,
     tg, og, tu, ou, rw, rg,
     gate, up, sg, su, router,
-    train, other, turned, blocks, first, firsts, local, parts, scales, tile,
-    load_sem, send_sem, recv_sem, own_sem,
+    train, other, turned, blocks, first, firsts, local, parts, scales, tiles, weight, gain,
+    load_sem, small_sem, send_sem, recv_sem, own_sem,
     first_send, first_recv, part_send, part_recv, scale_send, scale_recv,
     tile_send, tile_recv, pair_send, pair_recv, row_send, row_recv,
 ):
@@ -35,7 +35,6 @@
     strips = width // LANES
     zl, x, zh, y, c = (lax.axis_index(a) for a in AXES)
     me = (zh * ny + y) * nc + c
-    part = zl * nx + x
     arrays = ((tg, og, gate), (tu, ou, up))
 
     def load(t, e):
@@ -62,6 +61,12 @@
     for t in range(2):
         for copy in load(t, 0):
             copy.start()
+    small = (
+        pltpu.make_async_copy(rw, weight, small_sem.at[0]),
+        pltpu.make_async_copy(rg, gain, small_sem.at[1]),
+    )
+    for copy in small:
+        copy.start()
 
     @pl.loop(1, experts)
     def _(e):
@@ -79,20 +84,30 @@
         top = largest(t, 0)
         for k in range(strips):
             first[t, k : k + 1, :] = top[:, k * LANES : (k + 1) * LANES]
-    tile[...] = (rw[...] * rg[...]).astype(tile.dtype)
-    firsts[me] = first[...]
+        firsts[t, me] = first[t]
+    for copy in small:
+        copy.wait()
+    tiles[zl] = (weight[...] * gain[...]).astype(tiles.dtype)
 
     pl.semaphore_wait(barrier, len(everyone))
-    for _, d in others:
-        pltpu.make_async_remote_copy(
-            first, firsts.at[me], first_send, first_recv, device_id=d, device_id_type=MESH
-        ).start()
-    rows = pl.ds(pl.multiple_of(part * 8, 8), 8)
-    for _, d in others:
-        pltpu.make_async_remote_copy(
-            tile, router.at[rows, mine], tile_send, tile_recv, device_id=d, device_id_type=MESH
-        ).start()
-    pltpu.make_async_copy(tile, router.at[rows, mine], own_sem.at[1]).start()
+    for t in range(2):
+        for _, d in others:
+            pltpu.make_async_remote_copy(
+                first.at[t], firsts.at[t, me], first_send.at[t], first_recv.at[t],
+                device_id=d, device_id_type=MESH,
+            ).start()
+    handed = pltpu.make_async_remote_copy(
+        tiles.at[zl], tiles.at[zl], pair_send, pair_recv, device_id=across, device_id_type=MESH
+    )
+    handed.start()
+
+    def turn(t, e):
+        for k in range(strips):
+            lanes = slice(k * LANES, (k + 1) * LANES)
+            latest = train[t, e, :, lanes] + other[t, e, :, lanes].astype(jnp.float32)
+            turned[t, lanes, :] = latest.T
+
+    turn(0, 0)
 
     @pl.loop(1, experts)
     def _(e):
@@ -115,37 +130,62 @@
             def _():
                 parts[me] = local[chunk]
 
+    def deliver(t, e):
+        chunk = t * experts + e
+        for p, d in others:
+            pltpu.make_async_remote_copy(
+                blocks.at[p, chunk], arrays[t][2].at[e, :, mine], send_sem, recv_sem,
+                device_id=d, device_id_type=MESH,
+            ).start()
+        pltpu.make_async_copy(
+            blocks.at[me, chunk], arrays[t][2].at[e, :, mine], own_sem.at[0]
+        ).start()
+
     def send(t, e):
         chunk = t * experts + e
-        scale = scales[chunk]
-        inverse = 1.0 / scale
+        inverse = 1.0 / scales[chunk]
         for k in range(strips):
             lanes = slice(k * LANES, (k + 1) * LANES)
             latest = train[t, e, :, lanes] + other[t, e, :, lanes].astype(jnp.float32)
             turned[t, lanes, :] = (latest * inverse[k : k + 1, :]).T
         for p in range(members):
             blocks[p, chunk] = turned[t, p * cut : (p + 1) * cut, :].astype(blocks.dtype)
-        for p, d in others:
-            pltpu.make_async_remote_copy(
-                blocks.at[p, chunk], arrays[t][2].at[e, :, mine], send_sem, recv_sem,
+        deliver(t, e)
+
+    def send_first(t):
+        got = firsts.at[t, pl.ds(0, members - 1)]
+        pltpu.make_async_copy(got, got, first_recv.at[t]).wait()
+        scale = jnp.max(firsts[t], axis=0)
+        scales[t * experts] = scale
+        inverse = (1.0 / scale).T
+        for p in range(members):
+            pieces, row = [], p * cut
+            while row < (p + 1) * cut:
+                k = row // LANES
+                end = min((k + 1) * LANES, (p + 1) * cut)
+                column = inverse[row - k * LANES : end - k * LANES, k : k + 1]
+                pieces.append(turned[t, row:end, :] * column)
+                row = end
+            blocks[p, t * experts] = jnp.concatenate(pieces, axis=0).astype(blocks.dtype)
+        deliver(t, 0)
+
+    handed.wait()
+    bands = [pl.ds(pl.multiple_of((h * nx + x) * 8, 8), 8) for h in range(nzl)]
+    for _, d in others:
+        for h, band in enumerate(bands):
+            pltpu.make_async_remote_copy(
+                tiles.at[h], router.at[band, mine], tile_send, tile_recv,
                 device_id=d, device_id_type=MESH,
             ).start()
-        pltpu.make_async_copy(
-            blocks.at[me, chunk], arrays[t][2].at[e, :, mine], own_sem.at[0]
-        ).start()
-
-    got = firsts.at[pl.ds(0, members - 1)]
-    pltpu.make_async_copy(got, got, first_recv).wait()
-    for t in range(2):
-        scales[t * experts] = jnp.max(firsts[:, t], axis=0)
-    send(0, 0)
-
-    row = router.at[rows, pl.ds(0, (members - 1) * LANES)]
-    pltpu.make_async_copy(row, row, tile_recv).wait()
-    pltpu.make_async_copy(tile, router.at[rows, mine], own_sem.at[1]).wait()
-    pltpu.make_async_remote_copy(
-        router.at[rows], router.at[rows], pair_send, pair_recv, device_id=across, device_id_type=MESH
-    ).start()
+    kept = [
+        pltpu.make_async_copy(tiles.at[h], router.at[band, mine], own_sem.at[1 + h])
+        for h, band in enumerate(bands)
+    ]
+    for copy in kept:
+        copy.start()
+    turn(1, 0)
+
+    send_first(0)
 
     owns = lax.rem(me, experts) != 0
 
@@ -160,16 +200,16 @@
                 device_id=d, device_id_type=MESH,
             ).start()
 
-    send(1, 0)
-
-    pltpu.make_async_remote_copy(
-        router.at[rows], router.at[rows], pair_send, pair_recv, device_id=across, device_id_type=MESH
-    ).wait()
+    send_first(1)
+
+    for copy in kept:
+        copy.wait()
+    row = router.at[pl.ds(0, nzl * 8), pl.ds(0, (members - 1) * LANES)]
+    pltpu.make_async_copy(row, row, tile_recv).wait()
     for d in along:
-        for h in range(nzl):
-            block = pl.ds(pl.multiple_of((h * nx + x) * 8, 8), 8)
-            pltpu.make_async_remote_copy(
-                router.at[block], router.at[block], row_send, row_recv, device_id=d, device_id_type=MESH
+        for band in bands:
+            pltpu.make_async_remote_copy(
+                router.at[band], router.at[band], row_send, row_recv, device_id=d, device_id_type=MESH
             ).start()
 
     @pl.loop(1, experts)
@@ -198,14 +238,14 @@
     def drain(ref, sem):
         pltpu.make_async_copy(ref, ref, sem).wait()
 
-    drain(firsts.at[pl.ds(0, members - 1)], first_send)
-    row = router.at[pl.ds(0, 8), pl.ds(0, (members - 1) * LANES)]
+    for t in range(2):
+        drain(firsts.at[t, pl.ds(0, members - 1)], first_send.at[t])
     drain(row, tile_send)
 
     @pl.when(owns)
     def _():
         drain(local.at[pl.ds(0, members - 3)], part_send)
-        drain(firsts.at[pl.ds(0, members - 1), 0], scale_send)
+        drain(firsts.at[0, pl.ds(0, members - 1)], scale_send)
 
     @pl.when(jnp.logical_not(owns))
     def _():
@@ -217,6 +257,24 @@
     drain(blocks.at[0], own_sem.at[0])
     drain(blocks.at[pl.ds(0, members - 1)], send_sem)
     drain(blocks.at[pl.ds(0, members - 1)], recv_sem)
+
+
+def finish(*refs):
+    n = len(refs) // 2
+    arrived, outs, sem = refs[:n], refs[n:-1], refs[-1]
+    copies = []
+    for source, out in zip(arrived, outs):
+        if len(source.shape) == 3:
+            pieces = [(source.at[e], out.at[e]) for e in range(source.shape[0])]
+        else:
+            pieces = [(source, out)]
+        copies += [
+            pltpu.make_async_copy(a, b, sem.at[len(copies) + k]) for k, (a, b) in enumerate(pieces)
+        ]
+    for copy in copies:
+        copy.start()
+    for copy in copies:
+        copy.wait()
 
 
 def per_device(sizes, train_gate, other_gate, train_up, other_up, router_weight, router_gain):
@@ -227,40 +285,53 @@
     strips = width // LANES
     chunks = 2 * experts
     dma, bf16, f32 = pltpu.SemaphoreType.DMA, jnp.bfloat16, jnp.float32
-    hbm = pl.BlockSpec(memory_space=pl.ANY)
+    hbm = pl.BlockSpec(memory_space=pltpu.HBM)
     vmem = pl.BlockSpec(memory_space=pltpu.VMEM)
-    gate, up, sg, su, router = pl.pallas_call(
+    shapes = (
+        ((experts, cut, depth * members), bf16),
+        ((experts, cut, depth * members), bf16),
+        ((experts, cut), f32),
+        ((experts, cut), f32),
+        ((8 * parts, depth * members), bf16),
+    )
+    operands = (train_gate, other_gate, train_up, other_up, router_weight.T, router_gain[None])
+    arrived = pl.pallas_call(
         functools.partial(kernel, sizes),
-        out_shape=(
-            jax.ShapeDtypeStruct((experts, cut, depth * members), bf16),
-            jax.ShapeDtypeStruct((experts, cut, depth * members), bf16),
-            jax.ShapeDtypeStruct((experts, cut), f32),
-            jax.ShapeDtypeStruct((experts, cut), f32),
-            jax.ShapeDtypeStruct((8 * parts, depth * members), bf16),
-        ),
-        in_specs=[hbm] * 4 + [vmem] * 2,
-        out_specs=(hbm, hbm, vmem, vmem, hbm),
+        out_shape=[pltpu.VMEM(*shape) for shape in shapes],
+        in_specs=[hbm] * 6,
+        out_specs=[vmem] * 5,
         scratch_shapes=[
             pltpu.VMEM((2, experts, depth, width), f32),
             pltpu.VMEM((2, experts, depth, width), bf16),
             pltpu.VMEM((2, width, depth), f32),
             pltpu.VMEM((members, chunks, cut, depth), bf16),
             pltpu.VMEM((2, strips, LANES), f32),
-            pltpu.VMEM((members, 2, strips, LANES), f32),
+            pltpu.VMEM((2, members, strips, LANES), f32),
             pltpu.VMEM((chunks, strips, LANES), f32),
             pltpu.VMEM((members, strips, LANES), f32),
             pltpu.VMEM((chunks, strips, LANES), f32),
-            pltpu.VMEM((8, depth), bf16),
-            dma((2, 2, experts)),
-            dma, dma, dma((2,)),
-            dma, dma, dma, dma, dma, dma((chunks,)),
+            pltpu.VMEM((sizes[0], 8, depth), bf16),
+            pltpu.VMEM((8, depth), f32),
+            pltpu.VMEM((1, depth), f32),
+            dma((2, 2, experts)), dma((2,)),
+            dma, dma, dma((1 + sizes[0],)),
+            dma((2,)), dma((2,)), dma, dma, dma, dma((chunks,)),
             dma, dma, dma, dma, dma, dma,
         ],
         compiler_params=pltpu.CompilerParams(
-            collective_id=0, has_side_effects=True, vmem_limit_bytes=40 * 2**20
+            collective_id=0, has_side_effects=True, vmem_limit_bytes=48 * 2**20
         ),
         name="regroup",
-    )(train_gate, other_gate, train_up, other_up, router_weight.T, router_gain[None])
+    )(*(pltpu.with_memory_space_constraint(a, pltpu.HBM) for a in operands))
+    gate, up, sg, su, router = pl.pallas_call(
+        finish,
+        out_shape=[jax.ShapeDtypeStruct(*shape) for shape in shapes],
+        in_specs=[vmem] * 5,
+        out_specs=[hbm] * 5,
+        scratch_shapes=[dma((2 * experts + 3,))],
+        compiler_params=pltpu.CompilerParams(vmem_limit_bytes=4 * 2**20),
+        name="finish",
+    )(*(pltpu.with_memory_space_constraint(a, pltpu.VMEM) for a in arrived))
     return gate.transpose(0, 2, 1), up.transpose(0, 2, 1), sg, su, router.T
 
 

time: 92.2 us -> 83.3 us (0.903)
  local copies, waits for them, and re-layouts: 10 us -> 0 us
  Pallas kernels: 81.3 us -> 82.6 us
    unnamed x13 -> x0, local copies, waits for them, and re-layouts: 10 us -> none
    pallas_call x1 -> x2, Pallas kernels: 81.3 us -> 82.6 us  [the longest x1 79.9 us: per_device(): pl.pallas_call(functools.partial(kernel, sizes), out_shape=[pltpu.VMEM(*s...]
where the time goes in v2:
time: 83.3 us; the launch traced here: 83.2 us
  Pallas kernels  82.6 us (99%)
    pallas_call x1, Pallas kernels, per_device(): pl.pallas_call(functools.partial(kernel, sizes), out_shape=[pltpu.VMEM(*s...  79.9 us
    pallas_call x1, Pallas kernels, per_device(): pl.pallas_call(finish, out_shape=[jax.ShapeDtypeStruct(*shape) for shape...  2.74 us

profile of v2, /device:TPU:1, one launch (start us, length us, event | category | flops | bytes accessed | tf_op | source)
XLA Modules:
  0.0 83.2 jit_solution(917768302714282435)
XLA Ops:
  0.6 79.9 %regroup.1 = (bf16[8,88,2048]{2,1,0:T(8,128)(2,1)S(1)}, bf16[8,88,2048]{2,1,0:T(8,128)(2,1)S(1)}, f32[8,88]{1,0:T(8,128)S(1)}, f32[8,88]{1,0:T(8,128)S(1)}, bf16[64,2048]{1,0:T(8,128)(2,1)S(1)}) custom-call(f32[8,128,1408]{2,1,0:T(8,128)} %tg.1, bf16[8,128,1408]{2,1,0:T(8,128)(2,1)} %og.1, f32[8,128,1408]{2,1,0:T(8,128)} %tu.1, bf16[8,128,1408]{2,1,0:T(8,128)(2,1)} %ou.1, ...), custom_call_target="tpu_custom_call" | custom-call | tf_op jit(solution)/shard_map/regroup/pallas_call | solution.py:298
  80.5 2.7 %finish.1 = (bf16[8,88,2048]{2,1,0:T(8,128)(2,1)}, bf16[8,88,2048]{2,1,0:T(8,128)(2,1)}, f32[8,88]{1,0:T(8,128)}, f32[8,88]{1,0:T(8,128)}, bf16[64,2048]{1,0:T(8,128)(2,1)}) custom-call(bf16[8,88,2048]{2,1,0:T(8,128)(2,1)S(1)} %get-tuple-element.15.refs_0_, bf16[8,88,2048]{2,1,0:T(8,128)(2,1)S(1)} %get-tuple-element.16.refs_1_, ...), custom_call_target="tpu_custom_call" | custom-call | tf_op jit(solution)/shard_map/finish/pallas_call | solution.py:326

commit v3 on v2

--- a/solution.py
+++ b/solution.py
@@ -14,8 +14,8 @@
 FSDP = ("zh", "y", "c")
 LANES = 128
 PEERS = (
-    (1, 1, 0), (3, 1, 0), (0, 1, 0), (2, 1, 0), (1, 0, 0), (3, 0, 0), (2, 0, 0),
-    (1, 1, 1), (3, 1, 1), (0, 1, 1), (2, 1, 1), (1, 0, 1), (3, 0, 1), (2, 0, 1), (0, 0, 1),
+    (2, 1, 1), (2, 1, 0), (1, 1, 1), (1, 1, 0), (3, 1, 1), (3, 1, 0), (0, 1, 1), (0, 1, 0),
+    (2, 0, 1), (2, 0, 0), (1, 0, 1), (1, 0, 0), (3, 0, 1), (3, 0, 0), (0, 0, 1),
 )
 
 

time: 83.3 us -> 81.8 us (0.982)
  Pallas kernels: 82.6 us -> 81 us
    pallas_call x1, Pallas kernels: 79.9 us -> 78.3 us  [per_device(): pl.pallas_call(functools.partial(kernel, sizes), out_shape=[pltpu.VMEM(*s...]
where the time goes in v3:
time: 81.8 us; the launch traced here: 81.7 us
  Pallas kernels  81 us (99%)
    pallas_call x1, Pallas kernels, per_device(): pl.pallas_call(functools.partial(kernel, sizes), out_shape=[pltpu.VMEM(*s...  78.3 us
    pallas_call x1, Pallas kernels, per_device(): pl.pallas_call(finish, out_shape=[jax.ShapeDtypeStruct(*shape) for shape...  2.74 us

profile of v3, /device:TPU:1, one launch (start us, length us, event | category | flops | bytes accessed | tf_op | source)
XLA Modules:
  0.0 81.7 jit_solution(9909343201242796605)
XLA Ops:
  0.6 78.3 %regroup.1 = (bf16[8,88,2048]{2,1,0:T(8,128)(2,1)S(1)}, bf16[8,88,2048]{2,1,0:T(8,128)(2,1)S(1)}, f32[8,88]{1,0:T(8,128)S(1)}, f32[8,88]{1,0:T(8,128)S(1)}, bf16[64,2048]{1,0:T(8,128)(2,1)S(1)}) custom-call(f32[8,128,1408]{2,1,0:T(8,128)} %tg.1, bf16[8,128,1408]{2,1,0:T(8,128)(2,1)} %og.1, f32[8,128,1408]{2,1,0:T(8,128)} %tu.1, bf16[8,128,1408]{2,1,0:T(8,128)(2,1)} %ou.1, ...), custom_call_target="tpu_custom_call" | custom-call | tf_op jit(solution)/shard_map/regroup/pallas_call | solution.py:298
  78.9 2.7 %finish.1 = (bf16[8,88,2048]{2,1,0:T(8,128)(2,1)}, bf16[8,88,2048]{2,1,0:T(8,128)(2,1)}, f32[8,88]{1,0:T(8,128)}, f32[8,88]{1,0:T(8,128)}, bf16[64,2048]{1,0:T(8,128)(2,1)}) custom-call(bf16[8,88,2048]{2,1,0:T(8,128)(2,1)S(1)} %get-tuple-element.15.refs_0_, bf16[8,88,2048]{2,1,0:T(8,128)(2,1)S(1)} %get-tuple-element.16.refs_1_, ...), custom_call_target="tpu_custom_call" | custom-call | tf_op jit(solution)/shard_map/finish/pallas_call | solution.py:326

commit v4 on v3

--- a/solution.py
+++ b/solution.py
@@ -25,7 +25,7 @@
     gate, up, sg, su, router,
     train, other, turned, blocks, first, firsts, local, parts, scales, tiles, weight, gain,
     load_sem, small_sem, send_sem, recv_sem, own_sem,
-    first_send, first_recv, part_send, part_recv, scale_send, scale_recv,
+    first_send, first_recv, part_send, part_recv, scale_send, scale_recv, hand_send,
     tile_send, tile_recv, pair_send, pair_recv, row_send, row_recv,
 ):
     nzl, nx, nzh, ny, nc = sizes
@@ -183,9 +183,8 @@
     ]
     for copy in kept:
         copy.start()
+    send_first(0)
     turn(1, 0)
-
-    send_first(0)
 
     owns = lax.rem(me, experts) != 0
 
@@ -194,11 +193,12 @@
         got = parts.at[pl.ds(0, members - 1)]
         pltpu.make_async_copy(got, got, part_recv).wait()
         scales[me] = jnp.max(parts[...], axis=0)
-        for _, d in others:
-            pltpu.make_async_remote_copy(
-                scales.at[me], scales.at[me], scale_send, scale_recv.at[me],
-                device_id=d, device_id_type=MESH,
-            ).start()
+        for (_, d), step in zip(others, PEERS):
+            if step[2] == 0 or step == PEERS[-1]:
+                pltpu.make_async_remote_copy(
+                    scales.at[me], scales.at[me], scale_send, scale_recv.at[me],
+                    device_id=d, device_id_type=MESH,
+                ).start()
 
     send_first(1)
 
@@ -212,6 +212,8 @@
                 router.at[band], router.at[band], row_send, row_recv, device_id=d, device_id_type=MESH
             ).start()
 
+    mate = others[-1][1]
+
     @pl.loop(1, experts)
     def _(e):
         for t in range(2):
@@ -223,6 +225,13 @@
                     scales.at[chunk], scales.at[chunk], scale_recv.at[chunk]
                 ).wait()
 
+                @pl.when(lax.rem(chunk, nc) == c)
+                def _():
+                    pltpu.make_async_remote_copy(
+                        scales.at[chunk], scales.at[chunk], hand_send, scale_recv.at[chunk],
+                        device_id=mate, device_id_type=MESH,
+                    ).start()
+
             send(t, e)
 
     for t, out in enumerate((sg, su)):
@@ -245,11 +254,19 @@
     @pl.when(owns)
     def _():
         drain(local.at[pl.ds(0, members - 3)], part_send)
-        drain(firsts.at[0, pl.ds(0, members - 1)], scale_send)
+        drain(firsts.at[0, pl.ds(0, members // nc)], scale_send)
 
     @pl.when(jnp.logical_not(owns))
     def _():
         drain(local.at[pl.ds(0, members - 2)], part_send)
+
+    for k in range(nc):
+        handed_on = 2 * len([e for e in range(1, experts) if e % nc == k])
+        for less in range(2):
+
+            @pl.when(jnp.logical_and(c == k, owns == (less == 1)))
+            def _(rows=handed_on - less):
+                drain(local.at[pl.ds(0, rows)], hand_send)
 
     count = nzl * (nx - 1) * 8
     drain(router.at[pl.ds(0, count)], row_send)
@@ -315,7 +332,7 @@
             pltpu.VMEM((1, depth), f32),
             dma((2, 2, experts)), dma((2,)),
             dma, dma, dma((1 + sizes[0],)),
-            dma((2,)), dma((2,)), dma, dma, dma, dma((chunks,)),
+            dma((2,)), dma((2,)), dma, dma, dma, dma((chunks,)), dma,
             dma, dma, dma, dma, dma, dma,
         ],
         compiler_params=pltpu.CompilerParams(

time: 81.8 us -> 81.5 us (level)
  no operation moved by 1% of the time
where the time goes in v4:
time: 81.5 us; the launch traced here: 81.4 us
  Pallas kernels  80.8 us (99%)
    pallas_call x1, Pallas kernels, per_device(): pl.pallas_call(functools.partial(kernel, sizes), out_shape=[pltpu.VMEM(*s...  78 us
    pallas_call x1, Pallas kernels, per_device(): pl.pallas_call(finish, out_shape=[jax.ShapeDtypeStruct(*shape) for shape...  2.74 us

profile of v4, /device:TPU:1, one launch (start us, length us, event | category | flops | bytes accessed | tf_op | source)
XLA Modules:
  0.0 81.4 jit_solution(9565006618433319132)
XLA Ops:
  0.6 78.0 %regroup.1 = (bf16[8,88,2048]{2,1,0:T(8,128)(2,1)S(1)}, bf16[8,88,2048]{2,1,0:T(8,128)(2,1)S(1)}, f32[8,88]{1,0:T(8,128)S(1)}, f32[8,88]{1,0:T(8,128)S(1)}, bf16[64,2048]{1,0:T(8,128)(2,1)S(1)}) custom-call(f32[8,128,1408]{2,1,0:T(8,128)} %tg.1, bf16[8,128,1408]{2,1,0:T(8,128)(2,1)} %og.1, f32[8,128,1408]{2,1,0:T(8,128)} %tu.1, bf16[8,128,1408]{2,1,0:T(8,128)(2,1)} %ou.1, ...), custom_call_target="tpu_custom_call" | custom-call | tf_op jit(solution)/shard_map/regroup/pallas_call | solution.py:315
  78.7 2.7 %finish.1 = (bf16[8,88,2048]{2,1,0:T(8,128)(2,1)}, bf16[8,88,2048]{2,1,0:T(8,128)(2,1)}, f32[8,88]{1,0:T(8,128)}, f32[8,88]{1,0:T(8,128)}, bf16[64,2048]{1,0:T(8,128)(2,1)}) custom-call(bf16[8,88,2048]{2,1,0:T(8,128)(2,1)S(1)} %get-tuple-element.15.refs_0_, bf16[8,88,2048]{2,1,0:T(8,128)(2,1)S(1)} %get-tuple-element.16.refs_1_, ...), custom_call_target="tpu_custom_call" | custom-call | tf_op jit(solution)/shard_map/finish/pallas_call | solution.py:343

commit v5 on v4

--- a/solution.py
+++ b/solution.py
@@ -26,7 +26,7 @@
     train, other, turned, blocks, first, firsts, local, parts, scales, tiles, weight, gain,
     load_sem, small_sem, send_sem, recv_sem, own_sem,
     first_send, first_recv, part_send, part_recv, scale_send, scale_recv, hand_send,
-    tile_send, tile_recv, pair_send, pair_recv, row_send, row_recv,
+    tile_send, tile_recv, core_send, core_recv, pair_send, pair_recv, row_send, row_recv,
 ):
     nzl, nx, nzh, ny, nc = sizes
     experts, depth, width = tg.shape
@@ -85,12 +85,12 @@
         for k in range(strips):
             first[t, k : k + 1, :] = top[:, k * LANES : (k + 1) * LANES]
         firsts[t, me] = first[t]
-    for copy in small:
-        copy.wait()
-    tiles[zl] = (weight[...] * gain[...]).astype(tiles.dtype)
-
-    pl.semaphore_wait(barrier, len(everyone))
-    for t in range(2):
+        if t == 0:
+            pl.semaphore_wait(barrier, len(everyone))
+        else:
+            for copy in small:
+                copy.wait()
+            tiles[zl] = (weight[...] * gain[...]).astype(tiles.dtype)
         for _, d in others:
             pltpu.make_async_remote_copy(
                 first.at[t], firsts.at[t, me], first_send.at[t], first_recv.at[t],
@@ -171,12 +171,13 @@
 
     handed.wait()
     bands = [pl.ds(pl.multiple_of((h * nx + x) * 8, 8), 8) for h in range(nzl)]
-    for _, d in others:
-        for h, band in enumerate(bands):
-            pltpu.make_async_remote_copy(
-                tiles.at[h], router.at[band, mine], tile_send, tile_recv,
-                device_id=d, device_id_type=MESH,
-            ).start()
+    for (_, d), step in zip(others, PEERS):
+        if step[2] == 0:
+            for h, band in enumerate(bands):
+                pltpu.make_async_remote_copy(
+                    tiles.at[h], router.at[band, mine], tile_send, tile_recv,
+                    device_id=d, device_id_type=MESH,
+                ).start()
     kept = [
         pltpu.make_async_copy(tiles.at[h], router.at[band, mine], own_sem.at[1 + h])
         for h, band in enumerate(bands)
@@ -202,20 +203,33 @@
 
     send_first(1)
 
+    mate = others[-1][1]
+    chips = members // nc
     for copy in kept:
         copy.wait()
-    row = router.at[pl.ds(0, nzl * 8), pl.ds(0, (members - 1) * LANES)]
+    row = router.at[pl.ds(0, nzl * 8), pl.ds(0, (chips - 1) * LANES)]
     pltpu.make_async_copy(row, row, tile_recv).wait()
-    for d in along:
+    for q in range(chips):
+        lanes = pl.ds(pl.multiple_of((q * nc + c) * LANES, LANES), LANES)
         for band in bands:
             pltpu.make_async_remote_copy(
-                router.at[band], router.at[band], row_send, row_recv, device_id=d, device_id_type=MESH
+                router.at[band, lanes], router.at[band, lanes], core_send, core_recv,
+                device_id=mate, device_id_type=MESH,
             ).start()
-
-    mate = others[-1][1]
+    half = router.at[pl.ds(0, nzl * 8), pl.ds(0, chips * LANES)]
 
     @pl.loop(1, experts)
     def _(e):
+        @pl.when(e == 2)
+        def _():
+            pltpu.make_async_copy(half, half, core_recv).wait()
+            for d in along:
+                for band in bands:
+                    pltpu.make_async_remote_copy(
+                        router.at[band], router.at[band], row_send, row_recv,
+                        device_id=d, device_id_type=MESH,
+                    ).start()
+
         for t in range(2):
             chunk = t * experts + e
 
@@ -250,6 +264,7 @@
     for t in range(2):
         drain(firsts.at[t, pl.ds(0, members - 1)], first_send.at[t])
     drain(row, tile_send)
+    drain(half, core_send)
 
     @pl.when(owns)
     def _():
@@ -333,7 +348,7 @@
             dma((2, 2, experts)), dma((2,)),
             dma, dma, dma((1 + sizes[0],)),
             dma((2,)), dma((2,)), dma, dma, dma, dma((chunks,)), dma,
-            dma, dma, dma, dma, dma, dma,
+            dma, dma, dma, dma, dma, dma, dma, dma,
         ],
         compiler_params=pltpu.CompilerParams(
             collective_id=0, has_side_effects=True, vmem_limit_bytes=48 * 2**20

time: 81.5 us -> 81.4 us (level)
  no operation moved by 1% of the time
where the time goes in v5:
time: 81.4 us; the launch traced here: 81.3 us
  Pallas kernels  80.6 us (99%)
    pallas_call x1, Pallas kernels, per_device(): pl.pallas_call(functools.partial(kernel, sizes), out_shape=[pltpu.VMEM(*s...  77.9 us
    pallas_call x1, Pallas kernels, per_device(): pl.pallas_call(finish, out_shape=[jax.ShapeDtypeStruct(*shape) for shape...  2.74 us

profile of v5, /device:TPU:1, one launch (start us, length us, event | category | flops | bytes accessed | tf_op | source)
XLA Modules:
  0.0 81.3 jit_solution(12485502612270703755)
XLA Ops:
  0.6 77.9 %regroup.1 = (bf16[8,88,2048]{2,1,0:T(8,128)(2,1)S(1)}, bf16[8,88,2048]{2,1,0:T(8,128)(2,1)S(1)}, f32[8,88]{1,0:T(8,128)S(1)}, f32[8,88]{1,0:T(8,128)S(1)}, bf16[64,2048]{1,0:T(8,128)(2,1)S(1)}) custom-call(f32[8,128,1408]{2,1,0:T(8,128)} %tg.1, bf16[8,128,1408]{2,1,0:T(8,128)(2,1)} %og.1, f32[8,128,1408]{2,1,0:T(8,128)} %tu.1, bf16[8,128,1408]{2,1,0:T(8,128)(2,1)} %ou.1, ...), custom_call_target="tpu_custom_call" | custom-call | tf_op jit(solution)/shard_map/regroup/pallas_call | solution.py:330
  78.5 2.7 %finish.1 = (bf16[8,88,2048]{2,1,0:T(8,128)(2,1)}, bf16[8,88,2048]{2,1,0:T(8,128)(2,1)}, f32[8,88]{1,0:T(8,128)}, f32[8,88]{1,0:T(8,128)}, bf16[64,2048]{1,0:T(8,128)(2,1)}) custom-call(bf16[8,88,2048]{2,1,0:T(8,128)(2,1)S(1)} %get-tuple-element.15.refs_0_, bf16[8,88,2048]{2,1,0:T(8,128)(2,1)S(1)} %get-tuple-element.16.refs_1_, ...), custom_call_target="tpu_custom_call" | custom-call | tf_op jit(solution)/shard_map/finish/pallas_call | solution.py:358

commit v6 on v5

--- a/solution.py
+++ b/solution.py
@@ -23,10 +23,10 @@
     sizes,
     tg, og, tu, ou, rw, rg,
     gate, up, sg, su, router,
-    train, other, turned, blocks, first, firsts, local, parts, scales, tiles, weight, gain,
+    train, other, turned, blocks, first, firsts, local, parts, scales, tiles, weight, gain, halves,
     load_sem, small_sem, send_sem, recv_sem, own_sem,
     first_send, first_recv, part_send, part_recv, scale_send, scale_recv, hand_send,
-    tile_send, tile_recv, core_send, core_recv, pair_send, pair_recv, row_send, row_recv,
+    tile_send, tile_recv, core_send, core_recv, swap_send, swap_recv, pair_send, pair_recv, row_send, row_recv,
 ):
     nzl, nx, nzh, ny, nc = sizes
     experts, depth, width = tg.shape
@@ -34,7 +34,9 @@
     cut = width // members
     strips = width // LANES
     zl, x, zh, y, c = (lax.axis_index(a) for a in AXES)
-    me = (zh * ny + y) * nc + c
+    chip = zh * ny + y
+    chips = members // nc
+    me = chip * nc + c
     arrays = ((tg, og, gate), (tu, ou, up))
 
     def load(t, e):
@@ -51,6 +53,7 @@
     others = [peer(step) for step in PEERS]
     across = (lax.rem(zl + 1, nzl), x, zh, y, c)
     along = [(zl, lax.rem(x + k, nx), zh, y, c) for k in range(1, nx)]
+    mate = others[-1][1]
     mine = pl.ds(pl.multiple_of(me * LANES, LANES), LANES)
 
     barrier = pltpu.get_barrier_semaphore()
@@ -84,18 +87,19 @@
         top = largest(t, 0)
         for k in range(strips):
             first[t, k : k + 1, :] = top[:, k * LANES : (k + 1) * LANES]
-        firsts[t, me] = first[t]
+        firsts[t, (me, chip)[t]] = first[t]
         if t == 0:
             pl.semaphore_wait(barrier, len(everyone))
         else:
             for copy in small:
                 copy.wait()
             tiles[zl] = (weight[...] * gain[...]).astype(tiles.dtype)
-        for _, d in others:
-            pltpu.make_async_remote_copy(
-                first.at[t], firsts.at[t, me], first_send.at[t], first_recv.at[t],
-                device_id=d, device_id_type=MESH,
-            ).start()
+        for (_, d), step in zip(others, PEERS):
+            if t == 0 or step[2] == 0:
+                pltpu.make_async_remote_copy(
+                    first.at[t], firsts.at[t, (me, chip)[t]], first_send.at[t], first_recv.at[t],
+                    device_id=d, device_id_type=MESH,
+                ).start()
     handed = pltpu.make_async_remote_copy(
         tiles.at[zl], tiles.at[zl], pair_send, pair_recv, device_id=across, device_id_type=MESH
     )
@@ -153,9 +157,13 @@
         deliver(t, e)
 
     def send_first(t):
-        got = firsts.at[t, pl.ds(0, members - 1)]
-        pltpu.make_async_copy(got, got, first_recv.at[t]).wait()
-        scale = jnp.max(firsts[t], axis=0)
+        if t == 0:
+            got = firsts.at[t, pl.ds(0, members - 1)]
+            pltpu.make_async_copy(got, got, first_recv.at[t]).wait()
+            scale = jnp.max(firsts[t], axis=0)
+        else:
+            swapped.wait()
+            scale = jnp.maximum(halves[0], halves[1])
         scales[t * experts] = scale
         inverse = (1.0 / scale).T
         for p in range(members):
@@ -185,6 +193,14 @@
     for copy in kept:
         copy.start()
     send_first(0)
+
+    got = firsts.at[1, pl.ds(0, chips - 1)]
+    pltpu.make_async_copy(got, got, first_recv.at[1]).wait()
+    halves[0] = jnp.max(firsts[1, 0:chips], axis=0)
+    swapped = pltpu.make_async_remote_copy(
+        halves.at[0], halves.at[1], swap_send, swap_recv, device_id=mate, device_id_type=MESH
+    )
+    swapped.start()
     turn(1, 0)
 
     owns = lax.rem(me, experts) != 0
@@ -203,8 +219,6 @@
 
     send_first(1)
 
-    mate = others[-1][1]
-    chips = members // nc
     for copy in kept:
         copy.wait()
     row = router.at[pl.ds(0, nzl * 8), pl.ds(0, (chips - 1) * LANES)]
@@ -262,7 +276,7 @@
         pltpu.make_async_copy(ref, ref, sem).wait()
 
     for t in range(2):
-        drain(firsts.at[t, pl.ds(0, members - 1)], first_send.at[t])
+        drain(firsts.at[t, pl.ds(0, (members, chips)[t] - 1)], first_send.at[t])
     drain(row, tile_send)
     drain(half, core_send)
 
@@ -345,10 +359,11 @@
             pltpu.VMEM((sizes[0], 8, depth), bf16),
             pltpu.VMEM((8, depth), f32),
             pltpu.VMEM((1, depth), f32),
+            pltpu.VMEM((2, strips, LANES), f32),
             dma((2, 2, experts)), dma((2,)),
             dma, dma, dma((1 + sizes[0],)),
             dma((2,)), dma((2,)), dma, dma, dma, dma((chunks,)), dma,
-            dma, dma, dma, dma, dma, dma, dma, dma,
+            dma, dma, dma, dma, dma, dma, dma, dma, dma, dma,
         ],
         compiler_params=pltpu.CompilerParams(
             collective_id=0, has_side_effects=True, vmem_limit_bytes=48 * 2**20

time: 81.4 us -> 81.1 us (level)
  no operation moved by 1% of the time
where the time goes in v6:
time: 81.1 us; the launch traced here: 81 us
  Pallas kernels  80.3 us (99%)
    pallas_call x1, Pallas kernels, per_device(): pl.pallas_call(functools.partial(kernel, sizes), out_shape=[pltpu.VMEM(*s...  77.6 us
    pallas_call x1, Pallas kernels, per_device(): pl.pallas_call(finish, out_shape=[jax.ShapeDtypeStruct(*shape) for shape...  2.74 us

profile of v6, /device:TPU:1, one launch (start us, length us, event | category | flops | bytes accessed | tf_op | source)
XLA Modules:
  0.0 81.0 jit_solution(15086977708371589814)
XLA Ops:
  0.6 77.6 %regroup.1 = (bf16[8,88,2048]{2,1,0:T(8,128)(2,1)S(1)}, bf16[8,88,2048]{2,1,0:T(8,128)(2,1)S(1)}, f32[8,88]{1,0:T(8,128)S(1)}, f32[8,88]{1,0:T(8,128)S(1)}, bf16[64,2048]{1,0:T(8,128)(2,1)S(1)}) custom-call(f32[8,128,1408]{2,1,0:T(8,128)} %tg.1, bf16[8,128,1408]{2,1,0:T(8,128)(2,1)} %og.1, f32[8,128,1408]{2,1,0:T(8,128)} %tu.1, bf16[8,128,1408]{2,1,0:T(8,128)(2,1)} %ou.1, ...), custom_call_target="tpu_custom_call" | custom-call | tf_op jit(solution)/shard_map/regroup/pallas_call | solution.py:344
  78.2 2.7 %finish.1 = (bf16[8,88,2048]{2,1,0:T(8,128)(2,1)}, bf16[8,88,2048]{2,1,0:T(8,128)(2,1)}, f32[8,88]{1,0:T(8,128)}, f32[8,88]{1,0:T(8,128)}, bf16[64,2048]{1,0:T(8,128)(2,1)}) custom-call(bf16[8,88,2048]{2,1,0:T(8,128)(2,1)S(1)} %get-tuple-element.15.refs_0_, bf16[8,88,2048]{2,1,0:T(8,128)(2,1)S(1)} %get-tuple-element.16.refs_1_, ...), custom_call_target="tpu_custom_call" | custom-call | tf_op jit(solution)/shard_map/finish/pallas_call | solution.py:373
